TPU v7x, 16 devices: a whole 2x2x2 slice. The times are simulated.
16 devices in a mesh: fsdp: 16 (over z, y, x, core).
Axes of the slice: x: 2, y: 2, z: 2, core: 2. Of those that a mesh axis runs over, the one named last changes fastest.
Arguments:
- x_layers: bfloat16 [2, 16, 2048, 768], P(None, 'fsdp')
- dy_top: bfloat16 [16, 2048, 768], P('fsdp')
- x_next: bfloat16 [16, 2048, 768], P('fsdp')
- w_up: bfloat16 [2, 768, 3072], replicated
- w_down: bfloat16 [2, 3072, 768], replicated
- acc_up: float32 [2, 768, 3072], P(None, 'fsdp')
- acc_down: float32 [2, 3072, 768], P(None, 'fsdp')
- master_up: float32 [2, 768, 3072], P(None, 'fsdp')
- master_down: float32 [2, 3072, 768], P(None, 'fsdp')
- mom_up: float32 [2, 768, 3072], P(None, 'fsdp')
- mom_down: float32 [2, 3072, 768], P(None, 'fsdp')
- var_up: float32 [2, 768, 3072], P(None, 'fsdp')
- var_down: float32 [2, 3072, 768], P(None, 'fsdp')
Outputs:
- output 1: float32 [2, 768, 3072], P(None, 'fsdp')
- output 2: float32 [2, 3072, 768], P(None, 'fsdp')
- output 3: float32 [2, 768, 3072], P(None, 'fsdp')
- output 4: float32 [2, 3072, 768], P(None, 'fsdp')
- output 5: float32 [2, 768, 3072], P(None, 'fsdp')
- output 6: float32 [2, 3072, 768], P(None, 'fsdp')
- output 7: bfloat16 [16, 2048, 768], P('fsdp')
All inputs are finite; a program needn't handle non-finite values.
Results may differ from a plain program's by a relative error of at most 0.00956.
Values are sent between devices in bfloat16 or wider.
A program may use at most 1 GiB of HBM per device.

v0:
```python
import jax
import jax.numpy as jnp
from jax import lax
from jax.sharding import PartitionSpec as P

MICRO_STEPS = 2
STEP_COUNT = 3
BETA_MOM = 0.9
BETA_VAR = 0.999
ADAM_EPS = 1e-6
WEIGHT_DECAY = 0.01
LEARN_RATE = 0.06


def lamb_update(grad_full, master, mom_prev, var_prev):
    mom_new = BETA_MOM * mom_prev + (1.0 - BETA_MOM) * grad_full
    var_new = BETA_VAR * var_prev + (1.0 - BETA_VAR) * grad_full * grad_full
    update = (mom_new / (1.0 - BETA_MOM ** STEP_COUNT)) / (jnp.sqrt(var_new / (1.0 - BETA_VAR ** STEP_COUNT)) + ADAM_EPS) + WEIGHT_DECAY * master
    return mom_new, var_new, update


def layer_backward(x_cur, d_cur, w_up_l, w_down_l, need_dx):
    pre_act = jnp.einsum('bsd,df->bsf', x_cur, w_up_l, preferred_element_type=jnp.float32)
    act_f32, gelu_vjp = jax.vjp(jax.nn.gelu, pre_act)
    act_bf = act_f32.astype(jnp.bfloat16)
    d_act = jnp.einsum('bsd,fd->bsf', d_cur, w_down_l, preferred_element_type=jnp.float32)
    d_pre = gelu_vjp(d_act)[0].astype(jnp.bfloat16)
    part_down = jnp.einsum('bsf,bsd->fd', act_bf, d_cur, preferred_element_type=jnp.float32).astype(jnp.bfloat16)
    part_up = jnp.einsum('bsd,bsf->df', x_cur, d_pre, preferred_element_type=jnp.float32).astype(jnp.bfloat16)
    d_next = None
    if need_dx:
        d_next = (d_cur.astype(jnp.float32) + jnp.einsum('bsf,df->bsd', d_pre, w_up_l, preferred_element_type=jnp.float32)).astype(jnp.bfloat16)
    return part_up, part_down, d_next


def solution(mesh):
    shard_rows = P(None, 'fsdp')
    shard_batch = P('fsdp')
    spec_whole = P()

    def local_step(x_layers, dy_top, x_next, w_up, w_down, acc_up, acc_down, master_up, master_down, mom_up, mom_down, var_up, var_down):
        layers = w_up.shape[0]
        results = [None] * layers
        new_weights = [None] * layers
        d_cur = dy_top
        for layer_id in reversed(range(layers)):
            part_up, part_down, d_cur = layer_backward(x_layers[layer_id], d_cur, w_up[layer_id], w_down[layer_id], layer_id > 0)
            sum_up = lax.psum_scatter(part_up, 'fsdp', scatter_dimension=0, tiled=True)
            sum_down = lax.psum_scatter(part_down, 'fsdp', scatter_dimension=0, tiled=True)
            grad_up = (acc_up[layer_id] + sum_up.astype(jnp.float32)) / MICRO_STEPS
            grad_down = (acc_down[layer_id] + sum_down.astype(jnp.float32)) / MICRO_STEPS
            mom_up_new, var_up_new, upd_up = lamb_update(grad_up, master_up[layer_id], mom_up[layer_id], var_up[layer_id])
            mom_down_new, var_down_new, upd_down = lamb_update(grad_down, master_down[layer_id], mom_down[layer_id], var_down[layer_id])
            sq_local = jnp.stack([jnp.sum(master_up[layer_id] * master_up[layer_id]), jnp.sum(upd_up * upd_up), jnp.sum(master_down[layer_id] * master_down[layer_id]), jnp.sum(upd_down * upd_down)])
            sq_total = lax.psum(sq_local, 'fsdp')
            up_new = master_up[layer_id] - LEARN_RATE * jnp.sqrt(sq_total[0] / sq_total[1]) * upd_up
            down_new = master_down[layer_id] - LEARN_RATE * jnp.sqrt(sq_total[2] / sq_total[3]) * upd_down
            results[layer_id] = (up_new, down_new, mom_up_new, mom_down_new, var_up_new, var_down_new)
            w_up_new = lax.all_gather(up_new.astype(jnp.bfloat16), 'fsdp', axis=0, tiled=True)
            w_down_new = lax.all_gather(down_new.astype(jnp.bfloat16), 'fsdp', axis=0, tiled=True)
            new_weights[layer_id] = (w_up_new, w_down_new)
        x_cur = x_next
        for layer_id in range(layers):
            pre_act = jnp.einsum('bsd,df->bsf', x_cur, new_weights[layer_id][0], preferred_element_type=jnp.float32)
            act_bf = jax.nn.gelu(pre_act).astype(jnp.bfloat16)
            mlp_out = jnp.einsum('bsf,fd->bsd', act_bf, new_weights[layer_id][1], preferred_element_type=jnp.float32)
            x_cur = (x_cur.astype(jnp.float32) + mlp_out).astype(jnp.bfloat16)
        stacked = tuple(jnp.stack([results[layer_id][field_id] for layer_id in range(layers)]) for field_id in range(6))
        return stacked + (x_cur,)

    return jax.shard_map(local_step, mesh=mesh, in_specs=(shard_rows, shard_batch, shard_batch, spec_whole, spec_whole) + (shard_rows,) * 8, out_specs=(shard_rows,) * 6 + (shard_batch,), check_vma=False)
```

profile of v0, /device:TPU:0, one launch (start us, length us, event | category | flops | bytes accessed | tf_op | source)
XLA Modules:
  0.0 572.3 jit_solution(13900803550821561748)
XLA Ops:
  7.2 17.6 %fusion.55 = f32[2048,3072]{1,0:T(8,128)} fusion(bf16[2,768,3072]{2,1,0:T(8,128)(2,1)} %param.16, bf16[2,1,2048,768]{3,2,1,0:T(8,128)(2,1)} %param.13), kind=kOutput, calls=%fused_computation.60 | convolution fusion | flops 9663676416 | bytes 33030144 | tf_op jit(solution)/shard_map/bsd,df->bsf/dot_general | solution.py:23
  24.8 29.8 %fusion.6 = bf16[2048,3072]{1,0:T(8,128)(2,1)} fusion(f32[2048,3072]{1,0:T(8,128)} %fusion.55, bf16[2,3072,768]{2,1,0:T(8,128)(2,1)S(1)} %copy-done.18, bf16[1,2048,768]{2,1,0:T(8,128)(2,1)} %param.14), kind=kOutput, calls=%fused_computation.12 | convolution fusion | flops 9789505536 | bytes 45613056 | tf_op jit(solution)/shard_map/bsd,fd->bsf/dot_general | solution.py:26
  54.6 16.0 %fusion.70 = bf16[768,3072]{0,1:T(8,128)(2,1)} fusion(bf16[2048,3072]{1,0:T(8,128)(2,1)} %fusion.6, bf16[2,1,2048,768]{3,2,1,0:T(8,128)(2,1)} %param.13), kind=kOutput, calls=%fused_computation.68 | convolution fusion | flops 9666035712 | bytes 20447232 | tf_op jit(solution)/shard_map/bsd,bsf->df/dot_general | solution.py:29
  70.6 6.6 %copy.52 = bf16[768,3072]{1,0:T(8,128)(2,1)} copy(bf16[768,3072]{0,1:T(8,128)(2,1)} %fusion.70) | data formatting | bytes 9437184
  77.2 0.0 reduce-scatter.9.cloned.1.call-start
  77.3 17.7 %fusion.49 = f32[2048,3072]{1,0:T(8,128)} fusion(bf16[2,768,3072]{2,1,0:T(8,128)(2,1)} %param.16, bf16[2,1,2048,768]{3,2,1,0:T(8,128)(2,1)} %param.13), kind=kOutput, calls=%fused_computation.55 | convolution fusion | flops 9663676416 | bytes 33030144 | tf_op jit(solution)/shard_map/bsd,df->bsf/dot_general | solution.py:23
  95.0 14.3 %fusion.43 = bf16[1,2048,768]{2,1,0:T(8,128)(2,1)S(1)} fusion(bf16[1,2048,768]{2,1,0:T(8,128)(2,1)S(1)} %copy-done.19, bf16[2048,3072]{1,0:T(8,128)(2,1)} %fusion.6, bf16[2,768,3072]{2,1,0:T(8,128)(2,1)} %param.16), kind=kOutput, calls=%fused_computation.50 | convolution fusion | flops 9668395008 | bytes 23592960 | tf_op jit(solution)/shard_map/bsf,df->bsd/dot_general | solution.py:32
  109.4 1.7 copy-done.20
  111.0 20.3 %fusion.48 = bf16[3072,768]{1,0:T(8,128)(2,1)} fusion(f32[2048,3072]{1,0:T(8,128)} %fusion.49, bf16[1,2048,768]{2,1,0:T(8,128)(2,1)S(1)} %fusion.43), kind=kOutput, calls=%fused_computation.53 | convolution fusion | flops 9722658816 | bytes 33030144 | tf_op jit(solution)/shard_map/bsf,bsd->fd/dot_general | solution.py:28
  131.3 0.0 reduce-scatter.11.cloned.1.call-start
  131.3 21.1 %fusion.47 = bf16[3072,768]{1,0:T(8,128)(2,1)} fusion(f32[2048,3072]{1,0:T(8,128)} %fusion.55, bf16[1,2048,768]{2,1,0:T(8,128)(2,1)} %param.14), kind=kOutput, calls=%fused_computation.52 | convolution fusion | flops 9722658816 | bytes 33030144 | tf_op jit(solution)/shard_map/bsf,bsd->fd/dot_general | solution.py:28
  152.5 0.0 reduce-scatter.13.cloned.1.call-start
  152.5 41.2 %fusion.65 = bf16[768,3072]{0,1:T(8,128)(2,1)} fusion(f32[2048,3072]{1,0:T(8,128)} %fusion.49, bf16[2,3072,768]{2,1,0:T(8,128)(2,1)} %param.17, bf16[1,2048,768]{2,1,0:T(8,128)(2,1)} %copy-done.20, bf16[2,1,2048,768]{3,2,1,0:T(8,128)(2,1)} %param.13), kind=kOutput, calls=%fused_computation.67 | convolution fusion | flops 19455541248 | bytes 40894464 | tf_op jit(solution)/shard_map/bsd,bsf->df/dot_general | solution.py:29
  193.7 6.6 %copy.50 = bf16[768,3072]{1,0:T(8,128)(2,1)} copy(bf16[768,3072]{0,1:T(8,128)(2,1)} %fusion.65) | data formatting | bytes 9437184
  200.3 0.2 all-gather.7.cloned.1.call-start
  200.5 1.0 copy-done.15
  201.6 0.9 fusion.147
  202.5 0.5 copy.58
  202.9 0.9 fusion.146
  203.8 1.6 copy.61
  205.4 2.1 fusion.145
  207.6 1.6 copy.60
  209.2 0.9 fusion.144
  210.1 1.7 copy.59
  211.8 1.5 copy.54
  213.4 2.7 copy.57
  216.1 2.7 copy.56
  218.8 2.7 copy.55
  221.5 2.0 fusion.104
  223.5 2.1 copy.53
  225.6 44.7 %reduce-scatter.11.cloned.1.call-done = bf16[192,768]{1,0:T(8,128)(2,1)} async-done(((bf16[3072,768]{1,0:T(8,128)(2,1)}), bf16[192,768]{1,0:T(8,128)(2,1)}) %reduce-scatter.11.cloned.1.call-update) | async-done | bytes 294928 | tf_op jit(solution)/shard_map/reduce_scatter | solution.py:49
  270.3 5.6 multiply_reduce_fusion.3
  275.9 3.8 multiply_reduce_fusion
  279.7 2.6 pad_maximum_fusion.7
  282.3 52.6 %reduce-scatter.13.cloned.1.call-done = bf16[48,3072]{1,0:T(8,128)(2,1)} async-done(((bf16[768,3072]{1,0:T(8,128)(2,1)}), bf16[48,3072]{1,0:T(8,128)(2,1)}) %reduce-scatter.13.cloned.1.call-update) | async-done | bytes 294928
  335.0 2.1 copy.51
  337.1 6.5 %multiply_reduce_fusion.1 = (f32[]{:T(128)}, f32[48,3072]{0,1:T(8,128)}, f32[1,48,3072]{1,2,0:T(8,128)}, f32[1,48,3072]{1,2,0:T(8,128)}, f32[]{:T(128)}) fusion(f32[1,48,3072]{1,2,0:T(8,128)S(1)} %copy.54, f32[1,48,3072]{1,2,0:T(8,128)} %copy.57, bf16[48,3072]{0,1:T(8,128)(2,1)} %copy.51, f32[1,48,3072]{1,2,0:T(8,128)} %copy.56, f32[1,48,3072]{1,2,0:T(8,128)} %copy.55), kind=kLoop, calls=%fused_computation.102 | loop fusion | flops 2949118 | bytes 4423688 | tf_op jit(solution)/shard_map/reduce_sum | solution.py:54
  343.6 2.6 pad_maximum_fusion.6
  346.2 31.8 %all-reduce = (f32[4]{0:T(128)S(1)}, f32[4]{0:T(128)S(1)}) all-reduce(f32[4]{0:T(128)S(1)} %pad_maximum_fusion.7, f32[4]{0:T(128)S(1)} %pad_maximum_fusion.6), channel_id=1, replica_groups=mesh['fsdp'=16] {'fsdp'}, use_global_device_ids=true, to_apply=%region_13.0 | all-reduce | flops 8 | bytes 64 | tf_op jit(solution)/shard_map/psum | solution.py:55
  378.0 0.7 fusion.148
  381.3 2.9 fusion.108
  384.3 0.0 all-gather.5.cloned.1.call-start
  385.7 3.0 fusion.98
  388.7 2.1 copy.46
  390.8 0.7 all-gather.11.cloned.1.call-update
  391.5 0.3 all-gather.9.cloned.1.call-start
  393.2 3.1 fusion.100
  396.3 2.1 copy.48
  398.5 2.8 copy.41
  401.2 2.7 copy.40
  403.9 1.3 copy.43
  405.2 2.8 copy.42
  408.0 1.3 copy.45
  409.3 1.3 copy.44
  410.6 2.5 pad_maximum_fusion.1
  413.0 2.8 pad_maximum_fusion.3
  415.9 1.1 pad_maximum_fusion
  417.0 1.6 pad_maximum_fusion.2
  418.5 3.4 all-gather.7.cloned.1.call-done
  421.9 38.8 %all-gather.5.cloned.1.call-done = bf16[768,3072]{1,0:T(8,128)(2,1)} async-done(((bf16[48,3072]{1,0:T(8,128)(2,1)}), bf16[768,3072]{1,0:T(8,128)(2,1)}) %all-gather.5.cloned.1.call-update) | async-done | bytes 4718608 | tf_op jit(solution)/shard_map/all_gather | solution.py:59
  460.7 26.4 %fusion.42 = bf16[1,2048,768]{2,1,0:T(8,128)(2,1)} fusion(bf16[1,2048,768]{2,1,0:T(8,128)(2,1)} %param.15, bf16[3072,768]{1,0:T(8,128)(2,1)} %all-gather.7.cloned.1.call-done, bf16[768,3072]{1,0:T(8,128)(2,1)} %all-gather.5.cloned.1.call-done), kind=kOutput, calls=%fused_computation.48 | convolution fusion | flops 19388694528 | bytes 15728640 | tf_op jit(solution)/shard_map/bsf,fd->bsd/dot_general | solution.py:66
  487.0 12.6 %all-gather.11.cloned.1.call-done = bf16[3072,768]{1,0:T(8,128)(2,1)} async-done(((bf16[192,768]{1,0:T(8,128)(2,1)}), bf16[3072,768]{1,0:T(8,128)(2,1)}) %all-gather.11.cloned.1.call-update) | async-done | bytes 4718608 | tf_op jit(solution)/shard_map/all_gather | solution.py:60
  499.6 38.9 %all-gather.9.cloned.1.call-done = bf16[768,3072]{1,0:T(8,128)(2,1)} async-done(((bf16[48,3072]{1,0:T(8,128)(2,1)}), bf16[768,3072]{1,0:T(8,128)(2,1)}) %all-gather.9.cloned.1.call-update) | async-done | bytes 4718608 | tf_op jit(solution)/shard_map/all_gather | solution.py:59
  538.5 26.5 %fusion.41 = bf16[1,2048,768]{2,1,0:T(8,128)(2,1)} fusion(bf16[1,2048,768]{2,1,0:T(8,128)(2,1)} %fusion.42, bf16[3072,768]{1,0:T(8,128)(2,1)} %all-gather.11.cloned.1.call-done, bf16[768,3072]{1,0:T(8,128)(2,1)} %all-gather.9.cloned.1.call-done), kind=kOutput, calls=%fused_computation.46 | convolution fusion | flops 19388694528 | bytes 15728640 | tf_op jit(solution)/shard_map/bsf,fd->bsd/dot_general | solution.py:66
  (51 shorter events, 0.3 us)
Async XLA Ops:
  7.2 216.3 %reduce-scatter.15.cloned.1.call-start = ((), (), s32[]{:S(2)}) async-start(), calls=%async_computation.11 | async-start | bytes 5013504
  7.2 17.6 %copy-start.18 = (bf16[2,3072,768]{2,1,0:T(8,128)(2,1)S(1)}, bf16[2,3072,768]{2,1,0:T(8,128)(2,1)}, u32[]{:S(2)}) copy-start(bf16[2,3072,768]{2,1,0:T(8,128)(2,1)} %param.17) | copy-start | bytes 28311556
  77.2 148.4 %reduce-scatter.9.cloned.1.call-start = ((), (), s32[]{:S(2)}) async-start(), calls=%async_computation.4 | async-start | bytes 5013504 | tf_op jit(solution)/shard_map/reduce_scatter | solution.py:49
  77.3 17.7 %copy-start.19 = (bf16[1,2048,768]{2,1,0:T(8,128)(2,1)S(1)}, bf16[1,2048,768]{2,1,0:T(8,128)(2,1)}, u32[]{:S(2)}) copy-start(bf16[1,2048,768]{2,1,0:T(8,128)(2,1)} %param.14) | copy-start | bytes 9437188
  109.4 1.7 copy-start.20
  131.3 139.0 %reduce-scatter.11.cloned.1.call-start = ((), (), s32[]{:S(2)}) async-start(), calls=%async_computation.5 | async-start | bytes 5013504 | tf_op jit(solution)/shard_map/reduce_scatter | solution.py:49
  152.5 182.5 %reduce-scatter.13.cloned.1.call-start = ((), (), s32[]{:S(2)}) async-start(), calls=%async_computation.10 | async-start | bytes 5013504
  200.3 1.3 copy-start.15
  200.3 2.6 copy-start.16
  200.3 221.6 %all-gather.7.cloned.1.call-start = ((), (), s32[]{:S(2)}) async-start(), calls=%async_computation.7 | async-start | bytes 5013504 | tf_op jit(solution)/shard_map/all_gather | solution.py:60
  203.8 5.4 copy-start.17
  270.3 5.6 copy-start.3
  270.3 5.6 copy-start.4
  270.3 5.6 copy-start.5
  270.3 5.6 copy-start.6
  384.3 76.4 %all-gather.5.cloned.1.call-start = ((), (), s32[]{:S(2)}) async-start(), calls=%async_computation.6 | async-start | bytes 5013504 | tf_op jit(solution)/shard_map/all_gather | solution.py:59
  390.8 108.8 %all-gather.11.cloned.1.call-start = ((), (), s32[]{:S(2)}) async-start(), calls=%async_computation.9 | async-start | bytes 5013504 | tf_op jit(solution)/shard_map/all_gather | solution.py:60
  391.5 146.9 %all-gather.9.cloned.1.call-start = ((), (), s32[]{:S(2)}) async-start(), calls=%async_computation.8 | async-start | bytes 5013504 | tf_op jit(solution)/shard_map/all_gather | solution.py:59
  393.2 10.7 %copy-start.1 = (f32[1,48,3072]{1,2,0:T(8,128)S(1)}, f32[1,48,3072]{1,2,0:T(8,128)}, u32[]{:S(2)}) copy-start(f32[1,48,3072]{1,2,0:T(8,128)} %get-tuple-element.31) | copy-start | bytes 1769476
  398.4 9.6 %copy-start = (f32[1,48,3072]{1,2,0:T(8,128)S(1)}, f32[1,48,3072]{1,2,0:T(8,128)}, u32[]{:S(2)}) copy-start(f32[1,48,3072]{1,2,0:T(8,128)} %get-tuple-element.30) | copy-start | bytes 1769476
  405.2 4.1 copy-start.2
  409.3 3.8 copy-start.7
  409.3 3.8 copy-start.8
  410.5 5.3 copy-start.13
  410.5 5.3 copy-start.14
  410.5 6.4 %copy-start.9 = (f32[1,48,3072]{2,1,0:T(8,128)S(1)}, f32[1,48,3072]{2,1,0:T(8,128)}, u32[]{:S(2)}) copy-start(f32[1,48,3072]{2,1,0:T(8,128)} %copy.43) | copy-start | bytes 1769476
  410.5 6.4 %copy-start.10 = (f32[1,48,3072]{2,1,0:T(8,128)S(1)}, f32[1,48,3072]{2,1,0:T(8,128)}, u32[]{:S(2)}) copy-start(f32[1,48,3072]{2,1,0:T(8,128)} %copy.42) | copy-start | bytes 1769476
  410.5 6.4 %copy-start.11 = (f32[1,48,3072]{2,1,0:T(8,128)S(1)}, f32[1,48,3072]{2,1,0:T(8,128)}, u32[]{:S(2)}) copy-start(f32[1,48,3072]{2,1,0:T(8,128)} %copy.45) | copy-start | bytes 1769476
  410.6 6.4 %copy-start.12 = (f32[1,48,3072]{2,1,0:T(8,128)S(1)}, f32[1,48,3072]{2,1,0:T(8,128)}, u32[]{:S(2)}) copy-start(f32[1,48,3072]{2,1,0:T(8,128)} %copy.44) | copy-start | bytes 1769476
Sparse Core Ops, SparseCore 0:
  77.3 63.2 reduce-scatter.14
  145.0 60.3 reduce-scatter.8
  209.8 60.3 reduce-scatter.10
  274.5 60.3 reduce-scatter.12
  384.4 37.4 all-gather.6
  424.0 36.6 all-gather.4
  462.9 36.6 all-gather.10
  501.8 36.6 all-gather.8
where the time goes:
time: 579 us; the launch traced here: 572 us
  matrix products  231 us (40%)
  waiting for transfers between devices  192 us (33%)
  local copies, waits for them, and re-layouts  57 us (10%)
  other arithmetic  40.1 us (7%)
  blocking collectives  31.8 us (5%)
  between operations  20.1 us (3%)
    all_gather x2, waiting for transfers between devices, local_step(): lax.all_gather(up_new.astype(jnp.bfloat16), 'fsdp', axis=0, tiled=True)  77.7 us
    dot_general x2, matrix products, layer_backward(): jnp.einsum('bsd,bsf->df', x_cur, d_pre, preferred_element_type=jnp.float32)  57.2 us
    unnamed x10, waiting for transfers between devices  53.4 us
    dot_general x2, matrix products, local_step(): jnp.einsum('bsf,fd->bsd', act_bf, new_weights[layer_id][1], preferred_ele...  52.9 us
    reduce_scatter x2, waiting for transfers between devices, local_step(): lax.psum_scatter(part_down, 'fsdp', scatter_dimension=0, tiled=True)  44.7 us
    dot_general x2, matrix products, layer_backward(): jnp.einsum('bsf,bsd->fd', act_bf, d_cur, preferred_element_type=jnp.float32)  41.3 us
    dot_general x2, matrix products, layer_backward(): jnp.einsum('bsd,df->bsf', x_cur, w_up_l, preferred_element_type=jnp.float32)  35.3 us
    unnamed x54, local copies, waits for them, and re-layouts  35.3 us
  transfers between devices with their start and end apart: 8, of which 6 were waited for; matrix products, arithmetic and copies ran while one was open for 37% of the time, Pallas kernels for 0%

commit v1 on v0

v1 whole, which is shorter than its diff:
```python
import functools

import jax
import jax.numpy as jnp
from jax import lax
from jax.experimental import pallas as pl
from jax.experimental.pallas import tpu as pltpu
from jax.sharding import PartitionSpec as P

MICRO_STEPS = 2
STEP_COUNT = 3
BETA_MOM = 0.9
BETA_VAR = 0.999
ADAM_EPS = 1e-6
WEIGHT_DECAY = 0.01
LEARN_RATE = 0.06
NDEV = 16
D, FF, TOK = 768, 3072, 2048
TILES = FF // D
MT = 512
PAIR = 384
UP_ROWS, DN_ROWS = D // NDEV, FF // NDEV
LANES, SUB = 128, 8
MESH = pl.DeviceIdType.MESH
F32 = jnp.float32
BF16 = jnp.bfloat16
HBM = pl.BlockSpec(memory_space=pl.ANY)
DMA = pltpu.SemaphoreType.DMA
ALL = slice(None)

KINDS = {'up': (UP_ROWS, FF, MT, TILES), 'dn': (DN_ROWS, D, D, 1)}
MATRIX = {('up', 0): 0, ('dn', 0): 1, ('up', 1): 2, ('dn', 1): 3}
DIM_ORDERS = ((0, 1, 2), (1, 2, 0), (2, 0, 1))
GELU_A, GELU_B = 0.7978845608028654, 0.035677408136300125
ROW_COL = (((1,), (1,)), ((), ()))
COL_COL = (((0,), (0,)), ((), ()))


def span(i, n):
    return pl.ds(pl.multiple_of(i * n, n), n)


def gelu_tanh(v):
    half = 0.5 * v
    return half + half * jnp.tanh(v * (GELU_A + GELU_B * (v * v)))


def gelu_parts(v):
    sq = v * v
    t = jnp.tanh(v * (GELU_A + GELU_B * sq))
    half = 0.5 + 0.5 * t
    slope = 0.5 * v * (1.0 - t * t) * (GELU_A + (3 * GELU_B) * sq)
    return v * half, half + slope


def step_kernel(*refs):
    (x_all, dy_hbm, x_hbm, w_up, w_dn, acc_up, acc_dn, mas_up, mas_dn, mom_up, mom_dn, var_up, var_dn,
     o_mas_up, o_mas_dn, o_mom_up, o_mom_dn, o_var_up, o_var_dn, o_x, o_wu, o_wd,
     wu, wd, r0u, r0d, q1u, q1d, q2u, q2d, q3u, q3d, stu, std, xa, dy, xb, ta, td, w1t, w2t, norms,
     ld_sem, x_sem, wt_sem, out_sem, w_sem, xo_sem, rs_send, rs_recv, ag_send, ag_recv, dd_send, dd_recv, nm_send, nm_recv) = refs
    whole = {'up': wu, 'dn': wd}
    recv0 = {'up': r0u, 'dn': r0d}
    recvs = {'up': (q1u, q2u, q3u), 'dn': (q1d, q2d, q3d)}
    state_in = {'up': (acc_up, mas_up, mom_up, var_up), 'dn': (acc_dn, mas_dn, mom_dn, var_dn)}
    state_out = {'up': (None, o_mas_up, o_mom_up, o_var_up), 'dn': (None, o_mas_dn, o_mom_dn, o_var_dn)}
    w_out = {'up': o_wu, 'dn': o_wd}

    me = lax.axis_index('fsdp')
    bits = (me // 8, (me // 4) % 2, (me // 2) % 2)
    core = me % 2
    partner = me + 1 - 2 * core
    neighbours = tuple(me + step * (1 - 2 * bit) for bit, step in zip(bits, (8, 4, 2)))

    def local(src, dst, sem):
        return pltpu.make_async_copy(src, dst, sem)

    def remote(src, dst, send, recv, device):
        return pltpu.make_async_remote_copy(src_ref=src, dst_ref=dst, send_sem=send, recv_sem=recv, device_id=(device,), device_id_type=MESH)

    def st_block(kind, layer, k):
        if kind == 'up':
            return stu.at[layer, k]
        return std.at[span(4 * layer + k, DN_ROWS)]

    def state_loads(kind, layer):
        return [local(state_in[kind][k].at[layer], st_block(kind, layer, k), ld_sem.at[MATRIX[kind, layer], k]) for k in range(4)]

    def state_store(kind, layer, k):
        return local(st_block(kind, layer, k), state_out[kind][k].at[layer], out_sem.at[MATRIX[kind, layer], k])

    def w_store(kind):
        return local(whole[kind].at[1], w_out[kind], w_sem.at[MATRIX[kind, 0]])

    x1_load = local(x_all.at[1, 0], xa, x_sem.at[0])
    dy_load = local(dy_hbm.at[0], dy, x_sem.at[1])
    x0_load = local(x_all.at[0, 0], xb, x_sem.at[2])
    xn_load = local(x_hbm.at[0], xa, x_sem.at[3])

    def tile_loads(t):
        layer, cols, slot = 1 - t // TILES, span(t % TILES, D), t % 2
        return (local(w_up.at[layer, :, cols], w1t.at[slot], wt_sem.at[0, slot]),
                local(w_dn.at[layer, cols], w2t.at[slot], wt_sem.at[1, slot]))

    def start(copies):
        for copy in copies:
            copy.start()

    def wait(copies):
        for copy in copies:
            copy.wait()

    start((x1_load,) + tile_loads(0) + (dy_load, x0_load))
    start(state_loads('up', 1) + state_loads('up', 0))

    barrier = pltpu.get_barrier_semaphore()

    def hello(k, carry):
        pl.semaphore_signal(barrier, inc=1, device_id=(lax.rem(me + k, NDEV),), device_id_type=MESH)
        return carry

    lax.fori_loop(1, NDEV, hello, 0)
    pl.semaphore_wait(barrier, NDEV - 1)

    def place(fixed):
        return tuple(fixed.get(d, ALL) for d in range(3))

    def rs_core(kind, layer, k):
        m, cols = MATRIX[kind, layer], span(k, D)
        return remote(whole[kind].at[layer, :, :, :, 1 - core, :, cols], recv0[kind].at[:, :, :, :, cols], rs_send.at[m, k, 0], rs_recv.at[m, k, 0], partner)

    def rs_copies(kind, layer, stage, k):
        m, cols, third = MATRIX[kind, layer], span(k, D), KINDS[kind][0] // 3
        copies = []
        for p, dims in enumerate(DIM_ORDERS):
            fixed = {d: bits[d] for d in dims[:stage]}
            fixed[dims[stage]] = 1 - bits[dims[stage]]
            src = recv0[kind].at[place(fixed) + (pl.ds(third * p, third), cols)]
            dst = recvs[kind][stage].at[(p,) + (ALL,) * (3 - stage) + (cols,)]
            sem = 1 + 3 * stage + p
            copies.append(remote(src, dst, rs_send.at[m, k, sem], rs_recv.at[m, k, sem], neighbours[dims[stage]]))
        return copies

    def rs_begin(kind, layer, k=0):
        rs_core(kind, layer, k).start()

    def rs_first(kind, layer, k=0):
        rs_core(kind, layer, k).wait()
        cols = span(k, D)

        def add(i, carry):
            z, y, x = i // 4, (i // 2) % 2, i % 2
            recv0[kind][z, y, x, :, cols] = recv0[kind][z, y, x, :, cols] + whole[kind][layer, z, y, x, core, :, cols]
            return carry

        lax.fori_loop(0, 8, add, 0)
        start(rs_copies(kind, layer, 0, k))

    def rs_next(kind, layer, stage, k=0):
        cols, third = span(k, D), KINDS[kind][0] // 3
        buf, got = recv0[kind], recvs[kind][stage]
        arriving = rs_copies(kind, layer, stage, k)
        for p, dims in enumerate(DIM_ORDERS):
            arriving[p].wait()
            free = [d for d in range(3) if d in dims[stage + 1:]]
            for i in range(2 ** len(free)):
                where = {d: bits[d] for d in dims[:stage + 1]}
                slot = []
                for j, d in enumerate(free):
                    where[d] = (i >> (len(free) - 1 - j)) & 1
                    slot.append(where[d])
                idx = place(where) + (pl.ds(third * p, third), cols)
                buf[idx] = buf[idx] + got[(p,) + tuple(slot) + (ALL, cols)]
        start(rs_copies(kind, layer, stage + 1, k))

    def lamb(kind, layer):
        m = MATRIX[kind, layer]
        rows, cols, wide, chunks = KINDS[kind]
        third, per_row = rows // 3, cols // wide
        buf, got = recv0[kind], recvs[kind][2]
        st = functools.partial(st_block, kind, layer)
        wait(state_loads(kind, layer))
        for k in range(chunks):
            wait(rs_copies(kind, layer, 2, k))
        zero = jnp.zeros((2 * SUB, wide), F32)
        w_sum, u_sum = zero, zero
        for p in range(3):
            def chunk(i, carry):
                w_acc, u_acc = carry
                row, cs = i // per_row, span(i % per_row, wide)
                near = span(row, 2 * SUB)
                at = (pl.ds(pl.multiple_of(third * p + row * 2 * SUB, 2 * SUB), 2 * SUB), cs)
                total = buf[bits + at].astype(F32) + got[p, near, cs].astype(F32)
                master = st(1)[at]
                grad = (st(0)[at] + total) / MICRO_STEPS
                mom = BETA_MOM * st(2)[at] + (1.0 - BETA_MOM) * grad
                var = BETA_VAR * st(3)[at] + (1.0 - BETA_VAR) * grad * grad
                upd = (mom / (1.0 - BETA_MOM ** STEP_COUNT)) / (jnp.sqrt(var / (1.0 - BETA_VAR ** STEP_COUNT)) + ADAM_EPS) + WEIGHT_DECAY * master
                st(0)[at] = upd
                st(2)[at] = mom
                st(3)[at] = var
                return w_acc + master * master, u_acc + upd * upd

            w_sum, u_sum = lax.fori_loop(0, (third // (2 * SUB)) * per_row, chunk, (w_sum, u_sum))

        def fold(v):
            tiles = [v[SUB * i:SUB * i + SUB, LANES * j:LANES * j + LANES] for i in range(2) for j in range(wide // LANES)]
            return functools.reduce(lambda a, b: a + b, tiles)

        norms[m, me, 0:SUB] = fold(w_sum)
        norms[m, me, SUB:2 * SUB] = fold(u_sum)
        start([state_store(kind, layer, k) for k in (2, 3)])

        def tell(k, carry):
            remote(norms.at[m, me], norms.at[m, me], nm_send.at[m], nm_recv.at[m], lax.rem(me + k, NDEV)).start()
            return carry

        lax.fori_loop(1, NDEV, tell, 0)

    def apply(kind, layer):
        m = MATRIX[kind, layer]
        rows, cols, wide, _ = KINDS[kind]
        st = functools.partial(st_block, kind, layer)
        others = norms.at[m, pl.ds(0, NDEV - 1)]
        wait([local(others, others, sem.at[m]) for sem in (nm_send, nm_recv)])
        sums = jnp.sum(norms[m], axis=0)
        total = [jnp.sum(jnp.sum(v, axis=0, keepdims=True), axis=1, keepdims=True) for v in (sums[0:SUB], sums[SUB:2 * SUB])]
        scale = LEARN_RATE * (jnp.sqrt(total[0]) / jnp.sqrt(total[1]))
        per_row = cols // wide

        def chunk(i, carry):
            at = (span(i // per_row, 2 * SUB), span(i % per_row, wide))
            new = st(1)[at] - scale * st(0)[at]
            st(1)[at] = new
            whole[kind][(layer,) + bits + (core,) + at] = new.astype(BF16)
            return carry

        lax.fori_loop(0, (rows // (2 * SUB)) * per_row, chunk, 0)
        state_store(kind, layer, 1).start()

    def ag_copies(kind, layer, stage):
        m, third = MATRIX[kind, layer], KINDS[kind][0] // 3
        copies = []
        for p, dims in enumerate(DIM_ORDERS):
            ref = whole[kind].at[(layer,) + place({d: bits[d] for d in dims[:3 - stage]}) + (core, pl.ds(third * p, third))]
            copies.append(remote(ref, ref, ag_send.at[m, stage, p], ag_recv.at[m, stage, p], neighbours[dims[2 - stage]]))
        return copies

    def own_pass(kind, layer):
        m = MATRIX[kind, layer]
        ref = whole[kind].at[(layer,) + bits + (core,)]
        return remote(ref, ref, dd_send.at[m, 3, 0], dd_recv.at[m, 3, 0], partner)

    def pass_copies(kind, layer, stage):
        m, third = MATRIX[kind, layer], KINDS[kind][0] // 3
        copies = []
        for p, dims in enumerate(DIM_ORDERS):
            fixed = {d: bits[d] for d in dims[:2 - stage]}
            fixed[dims[2 - stage]] = 1 - bits[dims[2 - stage]]
            ref = whole[kind].at[(layer,) + place(fixed) + (core, pl.ds(third * p, third))]
            copies.append(remote(ref, ref, dd_send.at[m, stage, p], dd_recv.at[m, stage, p], partner))
        return copies

    def ag_begin(kind, layer):
        start(ag_copies(kind, layer, 0))
        own_pass(kind, layer).start()

    def ag_next(kind, layer, stage):
        wait(ag_copies(kind, layer, stage))
        if stage < 2:
            start(ag_copies(kind, layer, stage + 1))
        start(pass_copies(kind, layer, stage))

    def ag_end(kind, layer):
        own_pass(kind, layer).wait()
        for stage in range(3):
            wait(pass_copies(kind, layer, stage))
        if layer == 1:
            w_store(kind).start()

    def hidden(x_ref, slot):
        def rows(i, carry):
            at = span(i, MT)
            pre = jnp.dot(x_ref[at, :], w1t[slot], preferred_element_type=F32)
            d_act = lax.dot_general(dy[at, :], w2t[slot], ROW_COL, preferred_element_type=F32)
            a, slope = gelu_parts(pre)
            ta[at, :] = a.astype(BF16)
            td[at, :] = (d_act * slope).astype(BF16)
            return carry

        lax.fori_loop(0, TOK // MT, rows, 0)

    def part_down(layer, f):
        def chunk(j, carry):
            out = lax.dot_general(ta[:, span(j, PAIR)], dy[...], COL_COL, preferred_element_type=F32)
            wd[layer, f // 2, f % 2, j] = out.astype(BF16).reshape(2, DN_ROWS, D)
            return carry

        lax.fori_loop(0, 2, chunk, 0)

    def part_up(layer, f, x_ref):
        def chunk(j, carry):
            out = lax.dot_general(x_ref[:, span(j, PAIR)], td[...], COL_COL, preferred_element_type=F32)
            wu[layer, j, :, :, :, :, span(f, D)] = out.astype(BF16).reshape(2, 2, 2, UP_ROWS, D)
            return carry

        lax.fori_loop(0, 2, chunk, 0)

    def back_input(slot):
        def rows(i, carry):
            at = span(i, MT)
            std[at, :] += lax.dot_general(td[at, :], w1t[slot], ROW_COL, preferred_element_type=F32)
            return carry

        lax.fori_loop(0, TOK // MT, rows, 0)

    def clear(i, carry):
        std[span(i, 64), :] = jnp.zeros((64, D), F32)
        return carry

    lax.fori_loop(0, TOK // 64, clear, 0)
    wait((x1_load, dy_load))

    def upper(f, carry):
        slot = f % 2
        wait(tile_loads(f))
        start(tile_loads(f + 1))
        hidden(xa, slot)

        @pl.when(f > 0)
        def _():
            rs_next('up', 1, 0, f - 1)

        part_up(1, f, xa)
        rs_begin('up', 1, f)
        part_down(1, f)
        rs_first('up', 1, f)

        @pl.when(f > 0)
        def _():
            rs_next('up', 1, 1, f - 1)

        back_input(slot)
        return carry

    lax.fori_loop(0, TILES, upper, 0)
    rs_begin('dn', 1)
    xn_load.start()

    def next_dy(i, carry):
        at = span(i, 64)
        dy[at, :] = (dy[at, :].astype(F32) + std[at, :]).astype(BF16)
        return carry

    lax.fori_loop(0, TOK // 64, next_dy, 0)
    rs_next('up', 1, 0, TILES - 1)
    start(state_loads('dn', 1) + state_loads('dn', 0))
    x0_load.wait()

    after_hidden = (
        lambda: (rs_next('up', 1, 1, TILES - 1), rs_first('dn', 1)),
        lambda: rs_next('dn', 1, 0),
        lambda: (rs_next('dn', 1, 1), ag_next('up', 1, 1)),
        lambda: apply('dn', 1),
    )
    after_down = (
        lambda: lamb('up', 1),
        lambda: ag_next('up', 1, 0),
        lambda: lamb('dn', 1),
        lambda: rs_begin('dn', 0),
    )
    after_up = (
        lambda: (apply('up', 1), ag_begin('up', 1)),
        None,
        None,
        lambda: ag_next('up', 1, 2),
    )

    def at_tile(f, steps):
        for k, step in enumerate(steps):
            if step is not None:
                @pl.when(f == k)
                def _(step=step):
                    step()

    def lower(f, carry):
        wait(tile_loads(TILES + f))

        @pl.when(f < TILES - 1)
        def _():
            start(tile_loads(TILES + 1 + f))

        hidden(xb, f % 2)

        @pl.when(f > 0)
        def _():
            rs_first('up', 0, f - 1)

        at_tile(f, after_hidden)
        part_down(0, f)

        @pl.when(f > 0)
        def _():
            rs_next('up', 0, 0, f - 1)

        at_tile(f, after_down)
        part_up(0, f, xb)

        @pl.when(f > 0)
        def _():
            rs_next('up', 0, 1, f - 1)

        at_tile(f, after_up)
        rs_begin('up', 0, f)
        return carry

    lax.fori_loop(0, TILES, lower, 0)
    last = TILES - 1
    rs_first('up', 0, last)
    rs_next('up', 0, 0, last)
    rs_first('dn', 0)
    rs_next('up', 0, 1, last)
    lamb('up', 0)
    ag_end('up', 1)
    rs_next('dn', 0, 0)
    apply('up', 0)
    ag_begin('up', 0)
    rs_next('dn', 0, 1)
    ag_next('up', 0, 0)
    lamb('dn', 0)
    ag_next('up', 0, 1)
    apply('dn', 0)
    ag_begin('dn', 0)
    ag_next('up', 0, 2)
    ag_next('dn', 0, 0)
    ag_end('up', 0)

    xn_load.wait()

    def up_part(base, act):
        def body(n, carry):
            w = wu[0, :, :, :, :, :, span(n, D)].reshape(D, D)
            pre = jnp.dot(xa[base:base + MT, :], w, preferred_element_type=F32)
            act[span(n, MT), :] = gelu_tanh(pre).astype(BF16)
            return carry

        lax.fori_loop(0, TILES, body, 0)

    def down_part(base, act):
        def body(i, carry):
            at = pl.ds(pl.multiple_of(base + i * 256, 256), 256)
            prod = None
            for n in range(TILES):
                w = wd[0, n // 2, n % 2].reshape(D, D)
                term = jnp.dot(act[pl.ds(pl.multiple_of(n * MT + i * 256, 256), 256), :], w, preferred_element_type=F32)
                prod = term if prod is None else prod + term
            xb[at, :] = (xa[at, :].astype(F32) + prod).astype(BF16)
            return carry

        lax.fori_loop(0, 2, body, 0)

    def x_store(half):
        rows = pl.ds(half * 2 * MT, 2 * MT)
        return local(xb.at[rows], o_x.at[rows], xo_sem.at[half])

    up_part(0, ta)
    ag_next('dn', 0, 1)
    up_part(MT, td)
    ag_next('dn', 0, 2)
    ag_begin('dn', 1)
    ag_end('dn', 0)
    down_part(0, ta)
    ag_next('dn', 1, 0)
    down_part(MT, td)
    ag_next('dn', 1, 1)
    x_store(0).start()
    up_part(2 * MT, ta)
    up_part(3 * MT, td)
    ag_next('dn', 1, 2)
    down_part(2 * MT, ta)
    ag_end('dn', 1)
    down_part(3 * MT, td)
    x_store(1).start()
    wait([x_store(0), x_store(1), w_store('up'), w_store('dn')])
    for kind, layer in MATRIX:
        wait([state_store(kind, layer, k) for k in (1, 2, 3)])


def last_layer_kernel(x1, w_up, w_dn, *refs):
    ins, outs = refs[:6], refs[6:12]
    o_x, xv, xo, wu, wd, act, s0, s1, s2, s3, s4, s5, x_sem, w_sem, in_sem, out_sem = refs[12:]
    held = (s0, s1, s2, s3, s4, s5)
    first = pltpu.make_async_copy(x1, xv, x_sem.at[0])
    first.start()
    ups = [pltpu.make_async_copy(w_up.at[:, pl.ds(n * D, D)], wu.at[:, pl.ds(n * D, D)], w_sem.at[n]) for n in range(TILES)]
    downs = [pltpu.make_async_copy(w_dn.at[pl.ds(n * D, D)], wd.at[pl.ds(n * D, D)], w_sem.at[4 + n]) for n in range(TILES)]
    gets = [pltpu.make_async_copy(i, h, in_sem.at[k]) for k, (i, h) in enumerate(zip(ins, held))]
    puts = [pltpu.make_async_copy(h, o, out_sem.at[k]) for k, (h, o) in enumerate(zip(held, outs))]
    for copy in ups + downs + gets:
        copy.start()
    first.wait()
    for n in range(TILES):
        ups[n].wait()

        def rows(i, carry):
            at = span(i, MT)
            pre = jnp.dot(xv[at, :], wu[:, n * D:n * D + D], preferred_element_type=F32)
            act[at, n * D:n * D + D] = gelu_tanh(pre).astype(BF16)
            return carry

        lax.fori_loop(0, 4, rows, 0)
    for get, put in zip(gets, puts):
        get.wait()
        put.start()
    for copy in downs:
        copy.wait()
    sends = []
    for half in range(2):
        def body(i, carry):
            at = pl.ds(pl.multiple_of(half * 2 * MT + i * 256, 256), 256)
            out = jnp.dot(act[at, :], wd[...], preferred_element_type=F32)
            xo[at, :] = (xv[at, :].astype(F32) + out).astype(BF16)
            return carry

        lax.fori_loop(0, 4, body, 0)
        copy = pltpu.make_async_copy(xo.at[pl.ds(half * 2 * MT, 2 * MT)], o_x.at[0, pl.ds(half * 2 * MT, 2 * MT)], out_sem.at[6 + half])
        copy.start()
        sends.append(copy)
    for copy in puts + sends:
        copy.wait()


def whole_step(x_layers, dy_top, x_next, w_up, w_down, *states):
    cores = (2, 2, 2)
    sizes = [(r, c) for r, c, *_ in KINDS.values()]
    scratch = [pltpu.VMEM((2,) + cores + (2, r, c), BF16) for r, c in sizes]
    scratch += [pltpu.VMEM(cores + (r, c), BF16) for r, c in sizes]
    scratch += [pltpu.VMEM((3, 2, 2, r // 3, c), BF16) for r, c in sizes]
    scratch += [pltpu.VMEM((3, 2, r // 3, c), BF16) for r, c in sizes]
    scratch += [pltpu.VMEM((3, r // 3, c), BF16) for r, c in sizes]
    scratch += [pltpu.VMEM((2, 4, UP_ROWS, FF), F32), pltpu.VMEM((TOK, D), F32)]
    scratch += [pltpu.VMEM((TOK, D), BF16)] * 5
    scratch += [pltpu.VMEM((2, D, D), BF16)] * 2 + [pltpu.VMEM((4, NDEV, 16, 128), F32)]
    sem4 = (4, 4)
    rs_sem, ag_sem = DMA((4, TILES, 10)), DMA((4, 4, 3))
    scratch += [DMA(sem4), DMA((4,)), DMA(cores[1:]), DMA(sem4), DMA((2,)), DMA((2,)), rs_sem, rs_sem, ag_sem, ag_sem, ag_sem, ag_sem, DMA((4,)), DMA((4,))]
    state_shapes = [jax.ShapeDtypeStruct(s.shape, F32) for s in states[2:]]
    shapes = state_shapes + [jax.ShapeDtypeStruct((TOK, D), BF16)]
    shapes += [jax.ShapeDtypeStruct(cores + (2, r, c), BF16) for r, c in sizes]
    product = 2 * TOK * D * FF
    res = pl.pallas_call(
        step_kernel,
        out_shape=shapes,
        in_specs=[HBM] * 13,
        out_specs=[HBM] * 9,
        scratch_shapes=scratch,
        compiler_params=pltpu.CompilerParams(collective_id=0, has_side_effects=True, vmem_limit_bytes=67_000_000),
        cost_estimate=pl.CostEstimate(flops=11 * product, bytes_accessed=80_000_000, transcendentals=0),
        name='backward_update_gather',
    )(x_layers, dy_top, x_next, w_up, w_down, *states)
    x_mid, new_up, new_dn = res[6:]
    held = [pltpu.VMEM(s.shape, F32) for s in state_shapes]
    return pl.pallas_call(
        last_layer_kernel,
        out_shape=state_shapes + [jax.ShapeDtypeStruct(x_next.shape, BF16)],
        in_specs=[HBM] * 9,
        out_specs=[HBM] * 7,
        scratch_shapes=[pltpu.VMEM((TOK, D), BF16)] * 2 + [pltpu.VMEM((D, FF), BF16), pltpu.VMEM((FF, D), BF16), pltpu.VMEM((TOK, FF), BF16)] + held + [DMA((1,)), DMA((8,)), DMA((6,)), DMA((8,))],
        compiler_params=pltpu.CompilerParams(vmem_limit_bytes=60_000_000),
        cost_estimate=pl.CostEstimate(flops=2 * product, bytes_accessed=40_000_000, transcendentals=0),
        name='last_layer_forward',
    )(x_mid, new_up.reshape(D, FF), new_dn.reshape(FF, D), *res[:6])


def solution(mesh):
    shard_rows = P(None, 'fsdp')
    shard_batch = P('fsdp')
    spec_whole = P()

    def local_step(*args):
        return tuple(whole_step(*args))

    return jax.shard_map(local_step, mesh=mesh, in_specs=(shard_rows, shard_batch, shard_batch, spec_whole, spec_whole) + (shard_rows,) * 8, out_specs=(shard_rows,) * 6 + (shard_batch,), check_vma=False)
```

time: 579 us -> 272 us (0.47); the launches traced: 572 us -> 271 us
  Pallas kernels: 0 us -> 271 us
  matrix products: 231 us -> 0 us
  waiting for transfers between devices: 192 us -> 0 us
  local copies, waits for them, and re-layouts: 57 us -> 0 us
  other arithmetic: 40.1 us -> 0 us
  blocking collectives: 31.8 us -> 0 us
  between operations: 20.1 us -> 0.81 us
    pallas_call x0 -> x2, Pallas kernels: none -> 271 us  [the longest x1 237 us: whole_step(): pl.pallas_call(step_kernel, out_shape=shapes, in_specs=[HBM] * 13, out_sp...]
    dot_general x10 -> x0, matrix products: 231 us -> none  [the longest x2 57.2 us: layer_backward(): jnp.einsum('bsd,bsf->df', x_cur, d_pre, preferred_element_type=jnp.float32)]
    all_gather x4 -> x0, waiting for transfers between devices: 93.6 us -> none  [the longest x2 77.7 us: local_step(): lax.all_gather(up_new.astype(jnp.bfloat16), 'fsdp', axis=0, tiled=True)]
    unnamed x10 -> x0, waiting for transfers between devices: 53.4 us -> none
    reduce_scatter x2 -> x0, waiting for transfers between devices: 44.7 us -> none  [local_step(): lax.psum_scatter(part_down, 'fsdp', scatter_dimension=0, tiled=True)]
    unnamed x54 -> x0, local copies, waits for them, and re-layouts: 35.3 us -> none
    psum x1 -> x0, blocking collectives: 31.8 us -> none  [local_step(): sq_total = lax.psum(sq_local, 'fsdp')]
    reduce_sum x4 -> x0, other arithmetic: 18 us -> none  [the longest x2 10.3 us: local_step(): jnp.sum(upd_up * upd_up)]
  transfers between devices with their start and end apart: 8 -> 0, of which waited for: 6 -> 0; matrix products, arithmetic and copies ran while one was open for 37% -> 0% of each run, Pallas kernels for 0% -> 0%
where the time goes in v1:
time: 272 us; the launch traced here: 271 us
  Pallas kernels  271 us (100%)
    pallas_call x1, Pallas kernels, whole_step(): pl.pallas_call(step_kernel, out_shape=shapes, in_specs=[HBM] * 13, out_sp...  237 us
    pallas_call x1, Pallas kernels, whole_step(): pl.pallas_call(last_layer_kernel, out_shape=state_shapes + [jax.ShapeDtyp...  34.2 us

profile of v1, /device:TPU:0, one launch (start us, length us, event | category | flops | bytes accessed | tf_op | source)
XLA Modules:
  0.0 271.5 jit_solution(14930459660112539011)
XLA Ops:
  0.6 236.5 %backward_update_gather.1 = (f32[2,48,3072]{2,1,0:T(8,128)}, f32[2,192,768]{2,1,0:T(8,128)}, f32[2,48,3072]{2,1,0:T(8,128)}, f32[2,192,768]{2,1,0:T(8,128)}, f32...) custom-call(bf16[2,1,2048,768]{3,2,1,0:T(8,128)(2,1)} %refs_0_.1, ...), custom_call_target="tpu_custom_call" | custom-call | flops 106300440576 | bytes 80000000 | tf_op jit(solution)/shard_map/backward_update_gather/pallas_call | solution.py:550
  237.2 34.2 %last_layer_forward.1 = (f32[2,48,3072]{2,1,0:T(8,128)}, f32[2,192,768]{2,1,0:T(8,128)}, f32[2,48,3072]{2,1,0:T(8,128)}, f32[2,192,768]{2,1,0:T(8,128)}, f32[2,4...) custom-call(bf16[2048,768]{1,0:T(8,128)(2,1)} %get-tuple-element.16.x1, ...), custom_call_target="tpu_custom_call" | custom-call | flops 19327352832 | bytes 40000000 | tf_op jit(solution)/shard_map/last_layer_forward/pallas_call | solution.py:562

commit v2 on v1

--- a/solution.py
+++ b/solution.py
@@ -28,7 +28,7 @@
 DMA = pltpu.SemaphoreType.DMA
 ALL = slice(None)
 
-KINDS = {'up': (UP_ROWS, FF, MT, TILES), 'dn': (DN_ROWS, D, D, 1)}
+KINDS = {'up': (UP_ROWS, FF, MT, TILES), 'dn': (DN_ROWS, D, D, 2)}
 MATRIX = {('up', 0): 0, ('dn', 0): 1, ('up', 1): 2, ('dn', 1): 3}
 DIM_ORDERS = ((0, 1, 2), (1, 2, 0), (2, 0, 1))
 GELU_A, GELU_B = 0.7978845608028654, 0.035677408136300125
@@ -124,12 +124,15 @@
     def place(fixed):
         return tuple(fixed.get(d, ALL) for d in range(3))
 
+    def chunk_cols(kind, k):
+        return span(k, KINDS[kind][1] // KINDS[kind][3])
+
     def rs_core(kind, layer, k):
-        m, cols = MATRIX[kind, layer], span(k, D)
+        m, cols = MATRIX[kind, layer], chunk_cols(kind, k)
         return remote(whole[kind].at[layer, :, :, :, 1 - core, :, cols], recv0[kind].at[:, :, :, :, cols], rs_send.at[m, k, 0], rs_recv.at[m, k, 0], partner)
 
     def rs_copies(kind, layer, stage, k):
-        m, cols, third = MATRIX[kind, layer], span(k, D), KINDS[kind][0] // 3
+        m, cols, third = MATRIX[kind, layer], chunk_cols(kind, k), KINDS[kind][0] // 3
         copies = []
         for p, dims in enumerate(DIM_ORDERS):
             fixed = {d: bits[d] for d in dims[:stage]}
@@ -145,7 +148,7 @@
 
     def rs_first(kind, layer, k=0):
         rs_core(kind, layer, k).wait()
-        cols = span(k, D)
+        cols = chunk_cols(kind, k)
 
         def add(i, carry):
             z, y, x = i // 4, (i // 2) % 2, i % 2
@@ -156,7 +159,7 @@
         start(rs_copies(kind, layer, 0, k))
 
     def rs_next(kind, layer, stage, k=0):
-        cols, third = span(k, D), KINDS[kind][0] // 3
+        cols, third = chunk_cols(kind, k), KINDS[kind][0] // 3
         buf, got = recv0[kind], recvs[kind][stage]
         arriving = rs_copies(kind, layer, stage, k)
         for p, dims in enumerate(DIM_ORDERS):
@@ -333,17 +336,18 @@
         part_up(1, f, xa)
         rs_begin('up', 1, f)
         part_down(1, f)
+        back_input(slot)
         rs_first('up', 1, f)
 
         @pl.when(f > 0)
         def _():
             rs_next('up', 1, 1, f - 1)
 
-        back_input(slot)
         return carry
 
     lax.fori_loop(0, TILES, upper, 0)
-    rs_begin('dn', 1)
+    rs_begin('dn', 1, 0)
+    rs_begin('dn', 1, 1)
     xn_load.start()
 
     def next_dy(i, carry):
@@ -352,27 +356,24 @@
         return carry
 
     lax.fori_loop(0, TOK // 64, next_dy, 0)
-    rs_next('up', 1, 0, TILES - 1)
     start(state_loads('dn', 1) + state_loads('dn', 0))
     x0_load.wait()
 
+    last = TILES - 1
     after_hidden = (
-        lambda: (rs_next('up', 1, 1, TILES - 1), rs_first('dn', 1)),
-        lambda: rs_next('dn', 1, 0),
-        lambda: (rs_next('dn', 1, 1), ag_next('up', 1, 1)),
-        lambda: apply('dn', 1),
+        lambda: rs_next('up', 1, 0, last),
+        lambda: rs_next('dn', 1, 1, 0),
+        lambda: (rs_first('up', 0, 1), rs_next('dn', 1, 1, 1), ag_next('up', 1, 1)),
+        lambda: (rs_first('up', 0, 2), lamb('dn', 1), rs_next('up', 0, 0, 0), rs_next('up', 0, 0, 1)),
     )
     after_down = (
-        lambda: lamb('up', 1),
-        lambda: ag_next('up', 1, 0),
-        lambda: lamb('dn', 1),
-        lambda: rs_begin('dn', 0),
+        lambda: (rs_next('up', 1, 1, last), rs_first('dn', 1, 0), lamb('up', 1), rs_next('dn', 1, 0, 0), apply('up', 1)),
+        lambda: (rs_next('dn', 1, 0, 1), ag_next('up', 1, 0), rs_first('up', 0, 0)),
+        None,
+        lambda: (rs_next('up', 0, 0, 2), apply('dn', 1), rs_begin('dn', 0, 0), rs_begin('dn', 0, 1), ag_begin('dn', 1)),
     )
     after_up = (
-        lambda: (apply('up', 1), ag_begin('up', 1)),
-        None,
-        None,
-        lambda: ag_next('up', 1, 2),
+        lambda: (ag_begin('up', 1), rs_first('dn', 1, 1)),
     )
 
     def at_tile(f, steps):
@@ -390,48 +391,38 @@
             start(tile_loads(TILES + 1 + f))
 
         hidden(xb, f % 2)
-
-        @pl.when(f > 0)
-        def _():
-            rs_first('up', 0, f - 1)
-
         at_tile(f, after_hidden)
         part_down(0, f)
-
-        @pl.when(f > 0)
-        def _():
-            rs_next('up', 0, 0, f - 1)
-
         at_tile(f, after_down)
         part_up(0, f, xb)
-
-        @pl.when(f > 0)
-        def _():
-            rs_next('up', 0, 1, f - 1)
-
+        rs_begin('up', 0, f)
         at_tile(f, after_up)
-        rs_begin('up', 0, f)
         return carry
 
     lax.fori_loop(0, TILES, lower, 0)
-    last = TILES - 1
+    rs_next('up', 0, 1, 0)
+    rs_next('up', 0, 1, 1)
+    rs_next('up', 0, 1, 2)
+    rs_first('dn', 0, 0)
     rs_first('up', 0, last)
+    rs_first('dn', 0, 1)
     rs_next('up', 0, 0, last)
-    rs_first('dn', 0)
+    rs_next('dn', 0, 0, 0)
     rs_next('up', 0, 1, last)
+    rs_next('dn', 0, 0, 1)
     lamb('up', 0)
-    ag_end('up', 1)
-    rs_next('dn', 0, 0)
+    rs_next('dn', 0, 1, 0)
+    rs_next('dn', 0, 1, 1)
     apply('up', 0)
     ag_begin('up', 0)
-    rs_next('dn', 0, 1)
+    lamb('dn', 0)
     ag_next('up', 0, 0)
-    lamb('dn', 0)
-    ag_next('up', 0, 1)
     apply('dn', 0)
     ag_begin('dn', 0)
+    ag_next('up', 0, 1)
+    ag_next('dn', 0, 0)
     ag_next('up', 0, 2)
-    ag_next('dn', 0, 0)
+    ag_next('dn', 0, 1)
     ag_end('up', 0)
 
     xn_load.wait()
@@ -463,22 +454,22 @@
         return local(xb.at[rows], o_x.at[rows], xo_sem.at[half])
 
     up_part(0, ta)
-    ag_next('dn', 0, 1)
+    ag_next('up', 1, 2)
+    ag_next('dn', 1, 0)
     up_part(MT, td)
     ag_next('dn', 0, 2)
-    ag_begin('dn', 1)
+    ag_next('dn', 1, 1)
     ag_end('dn', 0)
     down_part(0, ta)
-    ag_next('dn', 1, 0)
     down_part(MT, td)
-    ag_next('dn', 1, 1)
     x_store(0).start()
     up_part(2 * MT, ta)
+    ag_end('up', 1)
     up_part(3 * MT, td)
     ag_next('dn', 1, 2)
     down_part(2 * MT, ta)
+    down_part(3 * MT, td)
     ag_end('dn', 1)
-    down_part(3 * MT, td)
     x_store(1).start()
     wait([x_store(0), x_store(1), w_store('up'), w_store('dn')])
     for kind, layer in MATRIX:
@@ -487,7 +478,7 @@
 
 def last_layer_kernel(x1, w_up, w_dn, *refs):
     ins, outs = refs[:6], refs[6:12]
-    o_x, xv, xo, wu, wd, act, s0, s1, s2, s3, s4, s5, x_sem, w_sem, in_sem, out_sem = refs[12:]
+    o_x, xv, xo, wu, wd, acc, s0, s1, s2, s3, s4, s5, x_sem, w_sem, in_sem, out_sem = refs[12:]
     held = (s0, s1, s2, s3, s4, s5)
     first = pltpu.make_async_copy(x1, xv, x_sem.at[0])
     first.start()
@@ -495,37 +486,39 @@
     downs = [pltpu.make_async_copy(w_dn.at[pl.ds(n * D, D)], wd.at[pl.ds(n * D, D)], w_sem.at[4 + n]) for n in range(TILES)]
     gets = [pltpu.make_async_copy(i, h, in_sem.at[k]) for k, (i, h) in enumerate(zip(ins, held))]
     puts = [pltpu.make_async_copy(h, o, out_sem.at[k]) for k, (h, o) in enumerate(zip(held, outs))]
-    for copy in ups + downs + gets:
+    for up, down in zip(ups, downs):
+        up.start()
+        down.start()
+    for copy in gets:
         copy.start()
     first.wait()
+
+    def x_store(i):
+        return pltpu.make_async_copy(xo.at[span(i, MT)], o_x.at[0, span(i, MT)], out_sem.at[6 + i])
+
     for n in range(TILES):
         ups[n].wait()
+        downs[n].wait()
 
         def rows(i, carry):
-            at = span(i, MT)
-            pre = jnp.dot(xv[at, :], wu[:, n * D:n * D + D], preferred_element_type=F32)
-            act[at, n * D:n * D + D] = gelu_tanh(pre).astype(BF16)
-            return carry
-
-        lax.fori_loop(0, 4, rows, 0)
-    for get, put in zip(gets, puts):
-        get.wait()
-        put.start()
-    for copy in downs:
-        copy.wait()
-    sends = []
-    for half in range(2):
-        def body(i, carry):
-            at = pl.ds(pl.multiple_of(half * 2 * MT + i * 256, 256), 256)
-            out = jnp.dot(act[at, :], wd[...], preferred_element_type=F32)
-            xo[at, :] = (xv[at, :].astype(F32) + out).astype(BF16)
-            return carry
-
-        lax.fori_loop(0, 4, body, 0)
-        copy = pltpu.make_async_copy(xo.at[pl.ds(half * 2 * MT, 2 * MT)], o_x.at[0, pl.ds(half * 2 * MT, 2 * MT)], out_sem.at[6 + half])
-        copy.start()
-        sends.append(copy)
-    for copy in puts + sends:
+            at, tile = span(i, MT), slice(n * D, n * D + D)
+            pre = jnp.dot(xv[at, :], wu[:, tile], preferred_element_type=F32)
+            out = jnp.dot(gelu_tanh(pre).astype(BF16), wd[tile, :], preferred_element_type=F32)
+            if n == 0:
+                acc[at, :] = xv[at, :].astype(F32) + out
+            elif n < TILES - 1:
+                acc[at, :] += out
+            else:
+                xo[at, :] = (acc[at, :] + out).astype(BF16)
+                x_store(i).start()
+            return carry
+
+        lax.fori_loop(0, TOK // MT, rows, 0)
+        if n == 1:
+            for get, put in zip(gets, puts):
+                get.wait()
+                put.start()
+    for copy in puts + [x_store(i) for i in range(TOK // MT)]:
         copy.wait()
 
 
@@ -564,7 +557,7 @@
         out_shape=state_shapes + [jax.ShapeDtypeStruct(x_next.shape, BF16)],
         in_specs=[HBM] * 9,
         out_specs=[HBM] * 7,
-        scratch_shapes=[pltpu.VMEM((TOK, D), BF16)] * 2 + [pltpu.VMEM((D, FF), BF16), pltpu.VMEM((FF, D), BF16), pltpu.VMEM((TOK, FF), BF16)] + held + [DMA((1,)), DMA((8,)), DMA((6,)), DMA((8,))],
+        scratch_shapes=[pltpu.VMEM((TOK, D), BF16)] * 2 + [pltpu.VMEM((D, FF), BF16), pltpu.VMEM((FF, D), BF16), pltpu.VMEM((TOK, D), F32)] + held + [DMA((1,)), DMA((8,)), DMA((6,)), DMA((10,))],
         compiler_params=pltpu.CompilerParams(vmem_limit_bytes=60_000_000),
         cost_estimate=pl.CostEstimate(flops=2 * product, bytes_accessed=40_000_000, transcendentals=0),
         name='last_layer_forward',

time: 272 us -> 253 us (0.930)
  Pallas kernels: 271 us -> 252 us
    pallas_call x1, Pallas kernels: 237 us -> 219 us  [whole_step(): pl.pallas_call(step_kernel, out_shape=shapes, in_specs=[HBM] * 13, out_sp...]
where the time goes in v2:
time: 253 us
  Pallas kernels  252 us (100%)
    pallas_call x1, Pallas kernels, whole_step(): pl.pallas_call(step_kernel, out_shape=shapes, in_specs=[HBM] * 13, out_sp...  219 us
    pallas_call x1, Pallas kernels, whole_step(): pl.pallas_call(last_layer_kernel, out_shape=state_shapes + [jax.ShapeDtyp...  33.6 us

profile of v2, /device:TPU:0, one launch (start us, length us, event | category | flops | bytes accessed | tf_op | source)
XLA Modules:
  0.0 253.2 jit_solution(2674767095333259269)
XLA Ops:
  0.6 218.8 %backward_update_gather.1 = (f32[2,48,3072]{2,1,0:T(8,128)}, f32[2,192,768]{2,1,0:T(8,128)}, f32[2,48,3072]{2,1,0:T(8,128)}, f32[2,192,768]{2,1,0:T(8,128)}, f32...) custom-call(bf16[2,1,2048,768]{3,2,1,0:T(8,128)(2,1)} %refs_0_.1, ...), custom_call_target="tpu_custom_call" | custom-call | flops 106300440576 | bytes 80000000 | tf_op jit(solution)/shard_map/backward_update_gather/pallas_call | solution.py:543
  219.5 33.6 %last_layer_forward.1 = (f32[2,48,3072]{2,1,0:T(8,128)}, f32[2,192,768]{2,1,0:T(8,128)}, f32[2,48,3072]{2,1,0:T(8,128)}, f32[2,192,768]{2,1,0:T(8,128)}, f32[2,4...) custom-call(bf16[2048,768]{1,0:T(8,128)(2,1)} %get-tuple-element.16.x1, ...), custom_call_target="tpu_custom_call" | custom-call | flops 19327352832 | bytes 40000000 | tf_op jit(solution)/shard_map/last_layer_forward/pallas_call | solution.py:555

commit v3 on v2

--- a/solution.py
+++ b/solution.py
@@ -57,7 +57,7 @@
     (x_all, dy_hbm, x_hbm, w_up, w_dn, acc_up, acc_dn, mas_up, mas_dn, mom_up, mom_dn, var_up, var_dn,
      o_mas_up, o_mas_dn, o_mom_up, o_mom_dn, o_var_up, o_var_dn, o_x, o_wu, o_wd,
      wu, wd, r0u, r0d, q1u, q1d, q2u, q2d, q3u, q3d, stu, std, xa, dy, xb, ta, td, w1t, w2t, norms,
-     ld_sem, x_sem, wt_sem, out_sem, w_sem, xo_sem, rs_send, rs_recv, ag_send, ag_recv, dd_send, dd_recv, nm_send, nm_recv) = refs
+     ld_sem, x_sem, first_sem, wt_sem, out_sem, w_sem, xo_sem, rs_send, rs_recv, ag_send, ag_recv, dd_send, dd_recv, nm_send, nm_recv) = refs
     whole = {'up': wu, 'dn': wd}
     recv0 = {'up': r0u, 'dn': r0d}
     recvs = {'up': (q1u, q2u, q3u), 'dn': (q1d, q2d, q3d)}
@@ -91,8 +91,10 @@
     def w_store(kind):
         return local(whole[kind].at[1], w_out[kind], w_sem.at[MATRIX[kind, 0]])
 
-    x1_load = local(x_all.at[1, 0], xa, x_sem.at[0])
-    dy_load = local(dy_hbm.at[0], dy, x_sem.at[1])
+    def first_loads(i):
+        at = span(i, MT)
+        return (local(x_all.at[1, 0, at], xa.at[at], first_sem.at[0, i]), local(dy_hbm.at[0, at], dy.at[at], first_sem.at[1, i]))
+
     x0_load = local(x_all.at[0, 0], xb, x_sem.at[2])
     xn_load = local(x_hbm.at[0], xa, x_sem.at[3])
 
@@ -109,8 +111,7 @@
         for copy in copies:
             copy.wait()
 
-    start((x1_load,) + tile_loads(0) + (dy_load, x0_load))
-    start(state_loads('up', 1) + state_loads('up', 0))
+    start(first_loads(0) + tile_loads(0) + first_loads(1))
 
     barrier = pltpu.get_barrier_semaphore()
 
@@ -280,8 +281,10 @@
         if layer == 1:
             w_store(kind).start()
 
-    def hidden(x_ref, slot):
+    def hidden(x_ref, slot, ready=None):
         def rows(i, carry):
+            if ready is not None:
+                ready(i)
             at = span(i, MT)
             pre = jnp.dot(x_ref[at, :], w1t[slot], preferred_element_type=F32)
             d_act = lax.dot_general(dy[at, :], w2t[slot], ROW_COL, preferred_element_type=F32)
@@ -321,13 +324,28 @@
         return carry
 
     lax.fori_loop(0, TOK // 64, clear, 0)
-    wait((x1_load, dy_load))
 
     def upper(f, carry):
         slot = f % 2
         wait(tile_loads(f))
+
+        def ready(i):
+            @pl.when(f == 0)
+            def _():
+                wait(first_loads(i))
+
+                @pl.when(i < 2)
+                def _():
+                    start(first_loads(i + 2))
+
+        hidden(xa, slot, ready)
         start(tile_loads(f + 1))
-        hidden(xa, slot)
+
+        @pl.when(f == 1)
+        def _():
+            x0_load.start()
+            start(state_loads('up', 1) + state_loads('up', 0))
+
 
         @pl.when(f > 0)
         def _():
@@ -480,18 +498,17 @@
     ins, outs = refs[:6], refs[6:12]
     o_x, xv, xo, wu, wd, acc, s0, s1, s2, s3, s4, s5, x_sem, w_sem, in_sem, out_sem = refs[12:]
     held = (s0, s1, s2, s3, s4, s5)
-    first = pltpu.make_async_copy(x1, xv, x_sem.at[0])
-    first.start()
+    def x_load(i):
+        return pltpu.make_async_copy(x1.at[span(i, MT)], xv.at[span(i, MT)], x_sem.at[i])
+
     ups = [pltpu.make_async_copy(w_up.at[:, pl.ds(n * D, D)], wu.at[:, pl.ds(n * D, D)], w_sem.at[n]) for n in range(TILES)]
     downs = [pltpu.make_async_copy(w_dn.at[pl.ds(n * D, D)], wd.at[pl.ds(n * D, D)], w_sem.at[4 + n]) for n in range(TILES)]
     gets = [pltpu.make_async_copy(i, h, in_sem.at[k]) for k, (i, h) in enumerate(zip(ins, held))]
     puts = [pltpu.make_async_copy(h, o, out_sem.at[k]) for k, (h, o) in enumerate(zip(held, outs))]
-    for up, down in zip(ups, downs):
-        up.start()
-        down.start()
-    for copy in gets:
-        copy.start()
-    first.wait()
+    x_load(0).start()
+    ups[0].start()
+    downs[0].start()
+    x_load(1).start()
 
     def x_store(i):
         return pltpu.make_async_copy(xo.at[span(i, MT)], o_x.at[0, span(i, MT)], out_sem.at[6 + i])
@@ -499,8 +516,18 @@
     for n in range(TILES):
         ups[n].wait()
         downs[n].wait()
+        if n < TILES - 1:
+            ups[n + 1].start()
+            downs[n + 1].start()
 
         def rows(i, carry):
+            if n == 0:
+                x_load(i).wait()
+
+                @pl.when(i < 2)
+                def _():
+                    x_load(i + 2).start()
+
             at, tile = span(i, MT), slice(n * D, n * D + D)
             pre = jnp.dot(xv[at, :], wu[:, tile], preferred_element_type=F32)
             out = jnp.dot(gelu_tanh(pre).astype(BF16), wd[tile, :], preferred_element_type=F32)
@@ -514,10 +541,13 @@
             return carry
 
         lax.fori_loop(0, TOK // MT, rows, 0)
-        if n == 1:
-            for get, put in zip(gets, puts):
+        if n in (1, 2):
+            for get, put in list(zip(gets, puts))[3 * n - 3:3 * n]:
                 get.wait()
                 put.start()
+        if n < 2:
+            for get in gets[3 * n:3 * n + 3]:
+                get.start()
     for copy in puts + [x_store(i) for i in range(TOK // MT)]:
         copy.wait()
 
@@ -535,7 +565,7 @@
     scratch += [pltpu.VMEM((2, D, D), BF16)] * 2 + [pltpu.VMEM((4, NDEV, 16, 128), F32)]
     sem4 = (4, 4)
     rs_sem, ag_sem = DMA((4, TILES, 10)), DMA((4, 4, 3))
-    scratch += [DMA(sem4), DMA((4,)), DMA(cores[1:]), DMA(sem4), DMA((2,)), DMA((2,)), rs_sem, rs_sem, ag_sem, ag_sem, ag_sem, ag_sem, DMA((4,)), DMA((4,))]
+    scratch += [DMA(sem4), DMA((4,)), DMA((2, 4)), DMA(cores[1:]), DMA(sem4), DMA((2,)), DMA((2,)), rs_sem, rs_sem, ag_sem, ag_sem, ag_sem, ag_sem, DMA((4,)), DMA((4,))]
     state_shapes = [jax.ShapeDtypeStruct(s.shape, F32) for s in states[2:]]
     shapes = state_shapes + [jax.ShapeDtypeStruct((TOK, D), BF16)]
     shapes += [jax.ShapeDtypeStruct(cores + (2, r, c), BF16) for r, c in sizes]
@@ -557,7 +587,7 @@
         out_shape=state_shapes + [jax.ShapeDtypeStruct(x_next.shape, BF16)],
         in_specs=[HBM] * 9,
         out_specs=[HBM] * 7,
-        scratch_shapes=[pltpu.VMEM((TOK, D), BF16)] * 2 + [pltpu.VMEM((D, FF), BF16), pltpu.VMEM((FF, D), BF16), pltpu.VMEM((TOK, D), F32)] + held + [DMA((1,)), DMA((8,)), DMA((6,)), DMA((10,))],
+        scratch_shapes=[pltpu.VMEM((TOK, D), BF16)] * 2 + [pltpu.VMEM((D, FF), BF16), pltpu.VMEM((FF, D), BF16), pltpu.VMEM((TOK, D), F32)] + held + [DMA((4,)), DMA((8,)), DMA((6,)), DMA((10,))],
         compiler_params=pltpu.CompilerParams(vmem_limit_bytes=60_000_000),
         cost_estimate=pl.CostEstimate(flops=2 * product, bytes_accessed=40_000_000, transcendentals=0),
         name='last_layer_forward',

time: 253 us -> 247 us (0.976)
  Pallas kernels: 252 us -> 247 us
    pallas_call x1, Pallas kernels: 33.6 us -> 29.5 us  [whole_step(): pl.pallas_call(last_layer_kernel, out_shape=state_shapes + [jax.ShapeDtyp...]
where the time goes in v3:
time: 247 us
  Pallas kernels  247 us (100%)
    pallas_call x1, Pallas kernels, whole_step(): pl.pallas_call(step_kernel, out_shape=shapes, in_specs=[HBM] * 13, out_sp...  217 us
    pallas_call x1, Pallas kernels, whole_step(): pl.pallas_call(last_layer_kernel, out_shape=state_shapes + [jax.ShapeDtyp...  29.5 us

profile of v3, /device:TPU:0, one launch (start us, length us, event | category | flops | bytes accessed | tf_op | source)
XLA Modules:
  0.0 247.4 jit_solution(7964713003875885630)
XLA Ops:
  0.6 217.1 %backward_update_gather.1 = (f32[2,48,3072]{2,1,0:T(8,128)}, f32[2,192,768]{2,1,0:T(8,128)}, f32[2,48,3072]{2,1,0:T(8,128)}, f32[2,192,768]{2,1,0:T(8,128)}, f32...) custom-call(bf16[2,1,2048,768]{3,2,1,0:T(8,128)(2,1)} %refs_0_.1, ...), custom_call_target="tpu_custom_call" | custom-call | flops 106300440576 | bytes 80000000 | tf_op jit(solution)/shard_map/backward_update_gather/pallas_call | solution.py:573
  217.7 29.5 %last_layer_forward.1 = (f32[2,48,3072]{2,1,0:T(8,128)}, f32[2,192,768]{2,1,0:T(8,128)}, f32[2,48,3072]{2,1,0:T(8,128)}, f32[2,192,768]{2,1,0:T(8,128)}, f32[2,4...) custom-call(bf16[2048,768]{1,0:T(8,128)(2,1)} %get-tuple-element.16.x1, ...), custom_call_target="tpu_custom_call" | custom-call | flops 19327352832 | bytes 40000000 | tf_op jit(solution)/shard_map/last_layer_forward/pallas_call | solution.py:585
